TPU v7x, 32 devices: a whole 2x2x4 slice. The times are simulated.
32 devices in a mesh: gx: 4 (over z), gy: 4 (over y, core), gz: 2 (over x).
Axes of the slice: x: 2, y: 2, z: 4, core: 2. Of those that a mesh axis runs over, the one named last changes fastest.
Arguments:
- point_data: float32 [1, 6, 16384], P(None, None, ('gx', 'gy', 'gz')), may hold values from -1 to 1
- neighbours: int32 [1, 64, 64, 64, 32], P(None, 'gx', 'gy', 'gz'), may hold values from 0 to 16383, as said below
- counts: int32 [1, 64, 64, 64], P(None, 'gx', 'gy', 'gz'), may hold values from 1 to 32, as said below
- kernel_in: bfloat16 [6, 80], replicated, may hold values from -2.5 to 2.5
- kernel_mid: bfloat16 [80, 80], replicated, may hold values from -0.625 to 0.625
- kernel_out: bfloat16 [80, 64], replicated, may hold values from -0.625 to 0.625
- spectral: bfloat16 [2, 16, 16, 16, 64, 64], P(None, 'gz', 'gx', 'gy'), may hold values from -48 to 48
- skip_weight: bfloat16 [64, 64], replicated, may hold values from -0.75 to 0.75
Outputs:
- latent_out: float32 [1, 64, 64, 64, 64], P(None, 'gx', 'gy', 'gz')
Inputs may be any that keep to these rules, and one draw needn't show every extreme that they name: `neighbours`: points are owned by location: point j of a geometry belongs to the device at position j // 512 in the order gx, gy, gz. Every neighbour of a node is owned by the node's own device or by a device whose gx, gy and gz indices each differ from it by at most one. Slots s >= counts of the node are padding that names some point all the same. `counts`: on every device some node of every geometry has all 32 slots valid.
All inputs are finite; a program needn't handle non-finite values.
Results may differ from a plain program's by a relative error of at most 0.02.
Values may be sent and summed in bfloat16 or wider, within the bound.
A program may use at most 128 MiB of HBM per device.

v0:
```python
import math

import jax
import jax.numpy as jnp
from jax import lax
from jax.sharding import PartitionSpec as P

GRID = 64
MODES = 16
NB = 32


HIGHEST = lax.Precision.HIGHEST
NORM_FLOOR = 1.0


def extended(cells, sides, width):
    for axis, dim in sides:
        count = lax.axis_size(axis)
        ends = count - 1
        head = lax.slice_in_dim(cells, 0, width, axis=dim)
        tail = lax.slice_in_dim(cells, cells.shape[dim] - width, cells.shape[dim], axis=dim)
        cells = jnp.concatenate(
            [
                lax.ppermute(tail, axis, [(i, (i + 1) % count) for i in range(ends)]),
                cells,
                lax.ppermute(head, axis, [((i + 1) % count, i) for i in range(ends)]),
            ],
            axis=dim,
        )
    return cells


def tables(length, keep_count, centred):
    position = jnp.arange(length, dtype=jnp.int32)
    frequency = jnp.arange(keep_count, dtype=jnp.int32)
    if centred:
        frequency = jnp.where(
            frequency < keep_count // 2, frequency, frequency + length - keep_count
        )
    phases = frequency[:, None] * position[None, :] % length
    angles = phases.astype(jnp.float32) * (2.0 * math.pi / length)
    return (jnp.cos(angles), jnp.sin(angles))


def third_weights(cos_table, sin_table, length):
    factor = (
        jnp.where(jnp.arange(cos_table.shape[0]) == 0, 1.0, 2.0).astype(jnp.float32)[:, None]
        / length**3
    )
    return (cos_table * factor, sin_table * factor)


def contract(pattern, operand, table):
    return jnp.einsum(pattern, operand, table, precision=HIGHEST)


def forward_real(values, cos_table, sin_table, pattern):
    return (contract(pattern, values, cos_table), -contract(pattern, values, sin_table))


def forward_complex(real_part, imag_part, cos_table, sin_table, pattern):
    new_real = contract(pattern, real_part, cos_table) + contract(pattern, imag_part, sin_table)
    new_imag = contract(pattern, imag_part, cos_table) - contract(pattern, real_part, sin_table)
    return (new_real, new_imag)


def inverse_complex(real_part, imag_part, cos_table, sin_table, pattern):
    new_real = contract(pattern, real_part, cos_table) - contract(pattern, imag_part, sin_table)
    new_imag = contract(pattern, real_part, sin_table) + contract(pattern, imag_part, cos_table)
    return (new_real, new_imag)


def inverse_real(real_part, imag_part, cos_table, sin_table, pattern):
    return contract(pattern, real_part, cos_table) - contract(pattern, imag_part, sin_table)


def kernel_mean(pair, valid, kernel_in, kernel_mid, kernel_out):
    hidden_one = jax.nn.gelu(
        jnp.dot(kernel_in.T, pair, preferred_element_type=jnp.float32), approximate=True
    ).astype(jnp.bfloat16)
    hidden_two = jax.nn.gelu(
        jnp.dot(kernel_mid.T, hidden_one, preferred_element_type=jnp.float32), approximate=True
    ).astype(jnp.bfloat16)
    values = jnp.dot(kernel_out.T, hidden_two, preferred_element_type=jnp.float32)
    values = values.reshape(values.shape[0], -1, NB)
    slots = jnp.arange(NB, dtype=jnp.int32)
    used = (slots[None, :] < valid[:, None]).astype(jnp.float32)
    total = jnp.sum(values * used[None], axis=2)
    return (total / valid.astype(jnp.float32)[None]).T.astype(jnp.bfloat16)


def split_exact(values):
    upper = values.astype(jnp.bfloat16)
    rest = values - upper.astype(jnp.float32)
    middle = rest.astype(jnp.bfloat16)
    lower = (rest - middle.astype(jnp.float32)).astype(jnp.bfloat16)
    return jnp.stack([upper, middle, lower], axis=1)


def body(point_data, neighbours, counts, kernel_in, kernel_mid, kernel_out, spectral, skip_weight):
    count_y = lax.axis_size("gy")
    count_z = lax.axis_size("gz")
    place_x = lax.axis_index("gx")
    place_y = lax.axis_index("gy")
    place_z = lax.axis_index("gz")
    geometry_count, cells_x, cells_y, cells_z = neighbours.shape[0:4]
    per_device = point_data.shape[2]
    channels = skip_weight.shape[0]
    beside_all = extended(point_data[None, None, None], (("gx", 0), ("gy", 1), ("gz", 2)), 1)
    table = jnp.transpose(beside_all, (3, 4, 0, 1, 2, 5)).reshape(
        geometry_count, point_data.shape[1], 27, per_device
    )
    pieces = split_exact(table).reshape(geometry_count, 3 * point_data.shape[1] * 27, per_device)
    owner = neighbours // per_device
    offset_z = owner % count_z - place_z + 1
    offset_y = owner // count_z % count_y - place_y + 1
    offset_x = owner // (count_z * count_y) - place_x + 1
    block_index = (offset_x * 3 + offset_y) * 3 + offset_z
    slot_index = neighbours % per_device
    centre_y = (
        (place_y * cells_y + jnp.arange(cells_y, dtype=jnp.int32)).astype(jnp.float32) + 0.5
    ) / GRID
    centre_z = (
        (place_z * cells_z + jnp.arange(cells_z, dtype=jnp.int32)).astype(jnp.float32) + 0.5
    ) / GRID
    row_y = jnp.broadcast_to(centre_y[:, None, None], (cells_y, cells_z, NB)).reshape(1, -1)
    row_z = jnp.broadcast_to(centre_z[None, :, None], (cells_y, cells_z, NB)).reshape(1, -1)
    slot_ids = jnp.arange(per_device, dtype=jnp.int32)[:, None]
    block_ids = jnp.arange(27, dtype=jnp.int32)[:, None]

    def one_slab(step):
        geometry = step // cells_x
        slab = step % cells_x
        rows = lax.dynamic_index_in_dim(pieces, geometry, 0, keepdims=False)
        blocks = lax.dynamic_index_in_dim(
            lax.dynamic_index_in_dim(block_index, geometry, 0, keepdims=False),
            slab,
            0,
            keepdims=False,
        ).reshape(1, -1)
        slots = lax.dynamic_index_in_dim(
            lax.dynamic_index_in_dim(slot_index, geometry, 0, keepdims=False),
            slab,
            0,
            keepdims=False,
        ).reshape(1, -1)
        valid = lax.dynamic_index_in_dim(
            lax.dynamic_index_in_dim(counts, geometry, 0, keepdims=False), slab, 0, keepdims=False
        ).reshape(-1)
        slot_hot = (slots == slot_ids).astype(jnp.bfloat16)
        found = jnp.dot(rows, slot_hot, preferred_element_type=jnp.float32).reshape(3, 6, 27, -1)
        found = found[0] + found[1] + found[2]
        block_hot = (blocks == block_ids).astype(jnp.float32)
        picked = jnp.sum(found * block_hot[None], axis=1)
        row_x = ((place_x * cells_x + slab).astype(jnp.float32) + 0.5) / GRID
        pair = jnp.concatenate(
            [picked[0:1] - row_x, picked[1:2] - row_y, picked[2:3] - row_z, picked[3:6]], axis=0
        ).astype(jnp.bfloat16)
        return kernel_mean(pair, valid, kernel_in, kernel_mid, kernel_out)

    latent = lax.map(one_slab, jnp.arange(geometry_count * cells_x, dtype=jnp.int32))
    latent = latent.reshape(geometry_count, cells_x, cells_y, cells_z, channels)
    cos_centred, sin_centred = tables(GRID, MODES, True)
    cos_third, sin_third = tables(GRID, MODES, False)
    back_cos, back_sin = third_weights(cos_third, sin_third, GRID)
    depth_full = lax.all_to_all(latent, "gz", split_axis=4, concat_axis=3, tiled=True)
    real_part, imag_part = forward_real(
        depth_full.astype(jnp.float32), cos_third, sin_third, "gxyzc,kz->gxykc"
    )
    real_part, imag_part = (
        lax.all_to_all(real_part, "gy", split_axis=3, concat_axis=2, tiled=True),
        lax.all_to_all(imag_part, "gy", split_axis=3, concat_axis=2, tiled=True),
    )
    real_part, imag_part = forward_complex(
        real_part, imag_part, cos_centred, sin_centred, "gxykc,jy->gxjkc"
    )
    real_part, imag_part = (
        lax.all_to_all(real_part, "gx", split_axis=2, concat_axis=1, tiled=True),
        lax.all_to_all(imag_part, "gx", split_axis=2, concat_axis=1, tiled=True),
    )
    real_part, imag_part = forward_complex(
        real_part, imag_part, cos_centred, sin_centred, "gxjkc,ix->gijkc"
    )
    spec_real, spec_imag = (
        lax.all_to_all(real_part, "gz", split_axis=1, concat_axis=4, tiled=True),
        lax.all_to_all(imag_part, "gz", split_axis=1, concat_axis=4, tiled=True),
    )
    spec_real = spec_real.astype(jnp.bfloat16)
    spec_imag = spec_imag.astype(jnp.bfloat16)
    mixed_real = jnp.einsum(
        "gijkc,ijkco->gijko", spec_real, spectral[0], preferred_element_type=jnp.float32
    ) - jnp.einsum("gijkc,ijkco->gijko", spec_imag, spectral[1], preferred_element_type=jnp.float32)
    mixed_imag = jnp.einsum(
        "gijkc,ijkco->gijko", spec_real, spectral[1], preferred_element_type=jnp.float32
    ) + jnp.einsum("gijkc,ijkco->gijko", spec_imag, spectral[0], preferred_element_type=jnp.float32)
    mixed_real = mixed_real.astype(jnp.bfloat16)
    mixed_imag = mixed_imag.astype(jnp.bfloat16)
    real_part, imag_part = (
        lax.all_to_all(mixed_real, "gz", split_axis=4, concat_axis=1, tiled=True),
        lax.all_to_all(mixed_imag, "gz", split_axis=4, concat_axis=1, tiled=True),
    )
    real_part, imag_part = inverse_complex(
        real_part.astype(jnp.float32),
        imag_part.astype(jnp.float32),
        cos_centred,
        sin_centred,
        "gijkc,ix->gxjkc",
    )
    real_part, imag_part = (
        lax.all_to_all(real_part, "gx", split_axis=1, concat_axis=2, tiled=True),
        lax.all_to_all(imag_part, "gx", split_axis=1, concat_axis=2, tiled=True),
    )
    real_part, imag_part = inverse_complex(
        real_part, imag_part, cos_centred, sin_centred, "gxjkc,jy->gxykc"
    )
    real_part, imag_part = (
        lax.all_to_all(real_part, "gy", split_axis=2, concat_axis=3, tiled=True),
        lax.all_to_all(imag_part, "gy", split_axis=2, concat_axis=3, tiled=True),
    )
    depth_part = inverse_real(real_part, imag_part, back_cos, back_sin, "gxykc,kz->gxyzc")
    branch = lax.all_to_all(depth_part, "gz", split_axis=3, concat_axis=4, tiled=True)
    skip = jnp.einsum("gxyzc,co->gxyzo", latent, skip_weight, preferred_element_type=jnp.float32)
    cells_total = float(GRID**3)
    mean = lax.psum(jnp.sum(branch, axis=(1, 2, 3)), ("gx", "gy", "gz")) / cells_total
    centred_branch = branch - mean[:, None, None, None, :]
    variance = (
        lax.psum(jnp.sum(centred_branch * centred_branch, axis=(1, 2, 3)), ("gx", "gy", "gz"))
        / cells_total
    )
    normed = centred_branch / jnp.sqrt(variance + NORM_FLOOR)[:, None, None, None, :]
    return jax.nn.gelu(normed + skip, approximate=True)


def solution(mesh):
    in_specs = (
        P(None, None, ("gx", "gy", "gz")),
        P(None, "gx", "gy", "gz", None),
        P(None, "gx", "gy", "gz"),
        P(),
        P(),
        P(),
        P(None, "gz", "gx", "gy", None, None),
        P(),
    )
    out_specs = P(None, "gx", "gy", "gz", None)
    return jax.shard_map(body, mesh=mesh, in_specs=in_specs, out_specs=out_specs, check_vma=False)
```

profile of v0, /device:TPU:0, one launch (start us, length us, event | category | flops | bytes accessed | tf_op | source)
XLA Modules:
  0.0 1652.7 jit_solution(1150132643046488185)
XLA Ops:
  42.2 1171.3 %while.13 = (s32[]{:T(128)}, bf16[16,512,64]{2,1,0:T(8,128)(2,1)}, s32[16]{0:T(128)S(1)}, s32[1,16,16,32,32]{4,3,2,1,0:T(8,128)}, bf16[1,486,512]{2,1,0:T(8,128)...) while((s32[]{:T(128)}, bf16[16,512,64]{2,1,0:T(8,128)(2,1)}, ...), condition=%wide.region_3.4_spmd.clone, body=%wide.region_0.3_spmd.clone.sunk | while | flops 8593375232 | bytes 135051792 | solution.py:162
  60.6 15.8 slice_add_fusion.3
  133.8 15.8 slice_add_fusion.3
  206.9 15.8 slice_add_fusion.3
  280.1 15.8 slice_add_fusion.3
  353.3 15.8 slice_add_fusion.3
  426.4 15.8 slice_add_fusion.3
  485.4 14.3 fusion.312
  499.6 15.8 slice_add_fusion.3
  572.8 15.8 slice_add_fusion.3
  645.9 15.8 slice_add_fusion.3
  719.1 15.8 slice_add_fusion.3
  778.0 14.3 fusion.312
  792.2 15.8 slice_add_fusion.3
  865.4 15.8 slice_add_fusion.3
  938.6 15.8 slice_add_fusion.3
  1011.7 15.8 slice_add_fusion.3
  1084.9 15.8 slice_add_fusion.3
  1158.1 15.8 slice_add_fusion.3
  1226.8 17.1 %all_to_all.201 = bf16[2,2,131072]{2,1,0:T(2,128)(2,1)S(1)} all-to-all(bf16[2,2,131072]{2,1,0:T(2,128)(2,1)S(1)} %reshape.420), channel_id=1, replica_groups=mesh['gx'=4,'gy'=4,'gz'=2] {'gz'}, dimensions={0} | all-to-all | bytes 2097152 | tf_op jit(solution)/shard_map/all_to_all | solution.py:167
  1469.2 29.1 %all_to_all.202 = f32[2,1,262144]{2,1,0:T(1,128)} all-to-all(f32[2,1,262144]{2,1,0:T(1,128)S(1)} %reshape.446), channel_id=1, replica_groups=mesh['gx'=4,'gy'=4,'gz'=2] {'gz'}, dimensions={0} | all-to-all | bytes 4194304 | tf_op jit(solution)/shard_map/all_to_all | solution.py:222
  1526.3 15.4 copy.232
  1548.5 39.2 %psum.14 = f32[1,64]{1,0:T(1,128)S(1)} all-reduce(f32[1,64]{1,0:T(1,128)S(1)} %reduce_sum.47), channel_id=1, replica_groups=mesh['gx'=4,'gy'=4,'gz'=2] {'gx','gy','gz'}, use_global_device_ids=true, to_apply=%region_5.6 | all-reduce | flops 64 | bytes 512 | tf_op jit(solution)/shard_map/psum | solution.py:225
  1597.1 40.2 %psum.15 = f32[1,64]{1,0:T(1,128)S(1)} all-reduce(f32[1,64]{1,0:T(1,128)S(1)} %reduce_sum.49), channel_id=1, replica_groups=mesh['gx'=4,'gy'=4,'gz'=2] {'gx','gy','gz'}, use_global_device_ids=true, to_apply=%region_7.8 | all-reduce | flops 64 | bytes 512 | tf_op jit(solution)/shard_map/psum | solution.py:228
  (544 shorter events, 1192.4 us)
Async XLA Ops:
  0.0 1646.3 %copy-start = (bf16[64,64]{1,0:T(8,128)(2,1)S(1)}, bf16[64,64]{1,0:T(8,128)(2,1)}, u32[]{:S(2)}) copy-start(bf16[64,64]{1,0:T(8,128)(2,1)} %param.17) | copy-start | bytes 24580
  0.0 20.5 %collective-permute-start = (f32[1,1,1,1,6,512]{5,0,4,3,2,1:T(1,128)}, f32[1,1,1,1,6,512]{5,0,4,3,2,1:T(1,128)S(1)}, u32[]{:S(2)}, u32[]{:S(2)}) collective-permute-start(f32[1,1,1,1,6,512]{5,0,4,3,2,1:T(1,128)} %bitcast.415), channel_id=1, source_target_pairs={{0,8},{8,16},{16,24},{1,9},{9,17},{17,25},{2,10},{10,18},{18,26},{... | collective-permute-start | bytes 36872 | tf_op jit(solution)/shard_map/ppermute | solution.py:25
  5.1 15.4 collective-permute-start.1
  6.4 14.1 copy-start.4
  20.5 21.7 %copy-start.3 = (bf16[80,64]{0,1:T(8,128)(2,1)S(1)}, bf16[80,64]{0,1:T(8,128)(2,1)}, u32[]{:S(2)}) copy-start(bf16[80,64]{0,1:T(8,128)(2,1)} %param.15) | copy-start | bytes 30724
  20.5 21.7 %copy-start.5 = (bf16[80,80]{1,0:T(8,128)(2,1)S(1)}, bf16[80,80]{1,0:T(8,128)(2,1)}, u32[]{:S(2)}) copy-start(bf16[80,80]{1,0:T(8,128)(2,1)} %param.14) | copy-start | bytes 38404
  20.5 21.7 %copy-start.6 = (bf16[6,80]{1,0:T(8,128)(2,1)S(1)}, bf16[6,80]{1,0:T(8,128)(2,1)}, u32[]{:S(2)}) copy-start(bf16[6,80]{1,0:T(8,128)(2,1)} %param.13) | copy-start | bytes 2884
  20.6 2.8 collective-permute-start.2
  22.1 4.7 collective-permute-start.3
  26.8 6.1 collective-permute-start.4
  30.2 7.1 collective-permute-start.5
  1275.5 14.2 all-to-all-start.1
  1289.7 12.3 all-to-all-start.2
  1312.7 11.9 all-to-all-start.3
  1324.6 9.6 all-to-all-start.4
  1337.1 7.1 all-to-all-start.5
  1344.2 8.0 all-to-all-start.6
  1358.7 7.1 all-to-all-start.8
  1365.8 7.1 all-to-all-start.7
  1375.7 9.3 all-to-all-start.10
  1385.0 9.8 all-to-all-start.9
  1406.6 14.2 all-to-all-start.12
  1420.8 12.3 all-to-all-start.11
  1637.3 9.0 copy-start.2
  (1 other events, 6.9 us)
where the time goes:
time: 1670 us; the launch traced here: 1650 us
  other arithmetic  526 us (31%)
  local copies, waits for them, and re-layouts  465 us (28%)
  matrix products  405 us (24%)
  blocking collectives  126 us (8%)
  starting transfers between devices  58.8 us (4%)
  loops' own time  36.1 us (2%)
  waiting for transfers between devices  35.4 us (2%)
    add x16, other arithmetic, one_slab(): found = found[0] + found[1] + found[2]  253 us
    dot_general x16, matrix products, one_slab(): jnp.dot(rows, slot_hot, preferred_element_type=jnp.float32)  228 us
    add x16, local copies, waits for them, and re-layouts, one_slab(): found = found[0] + found[1] + found[2]  161 us
    dot_general x16, local copies, waits for them, and re-layouts, kernel_mean(): jnp.dot(kernel_out.T, hidden_two, preferred_element_type=jnp.float32)  110 us
    reduce_sum x16, other arithmetic, one_slab(): picked = jnp.sum(found * block_hot[None], axis=1)  108 us
    reduce_sum x16, other arithmetic, kernel_mean(): total = jnp.sum(values * used[None], axis=2)  88.7 us
    dot_general x16, matrix products, kernel_mean(): jnp.dot(kernel_mid.T, hidden_one, preferred_element_type=jnp.float32)  69.7 us
    dot_general x20, matrix products, contract(): return jnp.einsum(pattern, operand, table, precision=HIGHEST)  49.3 us
  transfers between devices with their start and end apart: 18, of which 12 were waited for; matrix products, arithmetic and copies ran while one was open for 4% of the time, Pallas kernels for 0%

commit v1 on v0

v1 whole, which is shorter than its diff:
```python
import functools
import math

import jax
import jax.numpy as jnp
from jax import lax
from jax.experimental import pallas as pl
from jax.experimental.pallas import tpu as pltpu
from jax.sharding import PartitionSpec as P

GRID = 64
MODES = 16
NB = 32


HIGH = lax.Precision.HIGH
NORM_FLOOR = 1.0


def extended(cells, sides, width):
    for axis, dim in sides:
        count = lax.axis_size(axis)
        ends = count - 1
        head = lax.slice_in_dim(cells, 0, width, axis=dim)
        tail = lax.slice_in_dim(cells, cells.shape[dim] - width, cells.shape[dim], axis=dim)
        cells = jnp.concatenate(
            [
                lax.ppermute(tail, axis, [(i, (i + 1) % count) for i in range(ends)]),
                cells,
                lax.ppermute(head, axis, [((i + 1) % count, i) for i in range(ends)]),
            ],
            axis=dim,
        )
    return cells


def tables(length, keep_count, centred):
    position = jnp.arange(length, dtype=jnp.int32)
    frequency = jnp.arange(keep_count, dtype=jnp.int32)
    if centred:
        frequency = jnp.where(
            frequency < keep_count // 2, frequency, frequency + length - keep_count
        )
    phases = frequency[:, None] * position[None, :] % length
    angles = phases.astype(jnp.float32) * (2.0 * math.pi / length)
    return (jnp.cos(angles), jnp.sin(angles))


def third_weights(cos_table, sin_table, length):
    factor = (
        jnp.where(jnp.arange(cos_table.shape[0]) == 0, 1.0, 2.0).astype(jnp.float32)[:, None]
        / length**3
    )
    return (cos_table * factor, sin_table * factor)


def contract(pattern, operand, table):
    return jnp.einsum(pattern, operand, table, precision=HIGH)


def forward_real(values, cos_table, sin_table, pattern):
    return (contract(pattern, values, cos_table), -contract(pattern, values, sin_table))


def forward_complex(real_part, imag_part, cos_table, sin_table, pattern):
    new_real = contract(pattern, real_part, cos_table) + contract(pattern, imag_part, sin_table)
    new_imag = contract(pattern, imag_part, cos_table) - contract(pattern, real_part, sin_table)
    return (new_real, new_imag)


def inverse_complex(real_part, imag_part, cos_table, sin_table, pattern):
    new_real = contract(pattern, real_part, cos_table) - contract(pattern, imag_part, sin_table)
    new_imag = contract(pattern, real_part, sin_table) + contract(pattern, imag_part, cos_table)
    return (new_real, new_imag)


def inverse_real(real_part, imag_part, cos_table, sin_table, pattern):
    return contract(pattern, real_part, cos_table) - contract(pattern, imag_part, sin_table)


def gelu(v):
    inner = v * (0.7978845608028654 + 0.035677408136300125 * (v * v))
    half = 0.5 * v
    return half + half * jnp.tanh(inner)


def encoder_kernel(
    blocks, slots_ref, blocks_ref, counts_ref, centres_ref, table_ref, first_ref, mid_ref, last_ref, out_ref, total
):
    width = slots_ref.shape[1]
    per_device = table_ref.shape[1]
    rest_rows = table_ref.shape[0] - 8 * blocks
    slot_ids = lax.broadcasted_iota(jnp.int32, (per_device, width), 0).astype(jnp.int16)
    rest_ids = lax.broadcasted_iota(jnp.int32, (rest_rows, width), 0)
    rows = lax.broadcasted_iota(jnp.int32, (8, width), 0)
    counts = counts_ref[...]
    centres = centres_ref[...]
    total[...] = jnp.zeros_like(total)

    def step(s, carry):
        slot = jnp.broadcast_to(slots_ref[pl.ds(s, 1), :], (16, width)).astype(jnp.int16)
        slot = jnp.concatenate([slot] * (per_device // 16), axis=0)
        hot = jnp.where(slot_ids == slot, jnp.bfloat16(1), jnp.bfloat16(0))
        found = jnp.dot(table_ref[...], hot, preferred_element_type=jnp.float32)
        block = blocks_ref[pl.ds(s, 1), :]
        wide = jnp.broadcast_to(block, (8, width))
        picked = found[0:8]
        for b in range(1, blocks):
            picked = jnp.where(wide == b, found[8 * b : 8 * b + 8], picked)
        third = jnp.sum(jnp.where(rest_ids == block, found[8 * blocks :], 0.0), axis=0, keepdims=True)
        place = picked + pltpu.roll(picked, 4, 0) - centres
        pair = jnp.where(rows < 3, place, jnp.where(rows == 4, third, picked)).astype(jnp.bfloat16)
        hidden = gelu(jnp.dot(first_ref[...], pair, preferred_element_type=jnp.float32))
        hidden = gelu(
            jnp.dot(mid_ref[...], hidden.astype(jnp.bfloat16), preferred_element_type=jnp.float32)
        )
        hidden = hidden.astype(jnp.bfloat16).astype(jnp.float32)
        total[...] += jnp.where(s < counts, hidden, 0.0)
        return carry

    lax.fori_loop(0, slots_ref.shape[0], step, 0, unroll=4)
    mean = total[...] / counts.astype(jnp.float32)
    upper = mean.astype(jnp.bfloat16)
    lower = (mean - upper.astype(jnp.float32)).astype(jnp.bfloat16)
    last = last_ref[...]
    values = jnp.dot(last, upper, preferred_element_type=jnp.float32) + jnp.dot(
        last, lower, preferred_element_type=jnp.float32
    )
    out_ref[...] = values.T.astype(jnp.bfloat16)


def encode(slots, block_ids, counts, centres, table, first, mid, last):
    nodes = slots.shape[1]
    width = min(512, nodes)
    channels = last.shape[0]
    tile = lambda rows: pl.BlockSpec((rows, width), lambda i: (0, i))
    whole = lambda array: pl.BlockSpec(array.shape, lambda i: (0, 0))
    return pl.pallas_call(
        functools.partial(encoder_kernel, 27),
        grid=(nodes // width,),
        out_shape=jax.ShapeDtypeStruct((nodes, channels), jnp.bfloat16),
        in_specs=[tile(NB), tile(NB), tile(1), tile(8), whole(table), whole(first), whole(mid), whole(last)],
        out_specs=pl.BlockSpec((width, channels), lambda i: (i, 0)),
        scratch_shapes=[pltpu.VMEM((mid.shape[0], width), jnp.float32)],
    )(slots, block_ids, counts, centres, table, first, mid, last)


def packed_table(table):
    upper = table.astype(jnp.bfloat16)
    lower = (table - upper.astype(jnp.float32)).astype(jnp.bfloat16)
    main = jnp.concatenate([upper[0:3], upper[3:4], lower[0:3], upper[4:5]], axis=0)
    main = jnp.transpose(main, (1, 0, 2)).reshape(-1, table.shape[2])
    rows = jnp.concatenate([main, upper[5]], axis=0)
    return jnp.pad(rows, ((0, -rows.shape[0] % 128), (0, 0)))


def exchange(values, axis, split_axis, concat_axis):
    return lax.all_to_all(
        values.astype(jnp.bfloat16), axis, split_axis=split_axis, concat_axis=concat_axis, tiled=True
    ).astype(jnp.float32)


def body(point_data, neighbours, counts, kernel_in, kernel_mid, kernel_out, spectral, skip_weight):
    count_y = lax.axis_size("gy")
    count_z = lax.axis_size("gz")
    place_x = lax.axis_index("gx")
    place_y = lax.axis_index("gy")
    place_z = lax.axis_index("gz")
    geometry_count, cells_x, cells_y, cells_z = neighbours.shape[0:4]
    per_device = point_data.shape[2]
    channels = skip_weight.shape[0]
    beside_all = extended(point_data[None, None, None], (("gx", 0), ("gy", 1), ("gz", 2)), 1)
    table = jnp.transpose(beside_all, (3, 4, 0, 1, 2, 5)).reshape(
        geometry_count, point_data.shape[1], 27, per_device
    )
    owner = neighbours // per_device
    offset_z = owner % count_z - place_z + 1
    offset_y = owner // count_z % count_y - place_y + 1
    offset_x = owner // (count_z * count_y) - place_x + 1
    block_index = (offset_x * 3 + offset_y) * 3 + offset_z
    slot_index = neighbours % per_device
    centre_y = (
        (place_y * cells_y + jnp.arange(cells_y, dtype=jnp.int32)).astype(jnp.float32) + 0.5
    ) / GRID
    centre_z = (
        (place_z * cells_z + jnp.arange(cells_z, dtype=jnp.int32)).astype(jnp.float32) + 0.5
    ) / GRID
    centre_x = (
        (place_x * cells_x + jnp.arange(cells_x, dtype=jnp.int32)).astype(jnp.float32) + 0.5
    ) / GRID
    shape = (cells_x, cells_y, cells_z)
    centres = jnp.stack(
        [
            jnp.broadcast_to(centre_x[:, None, None], shape).reshape(-1),
            jnp.broadcast_to(centre_y[None, :, None], shape).reshape(-1),
            jnp.broadcast_to(centre_z[None, None, :], shape).reshape(-1),
        ]
    )
    centres = jnp.pad(centres, ((0, 5), (0, 0)))
    first = jnp.stack(
        [kernel_in[0], kernel_in[1], kernel_in[2], kernel_in[3], kernel_in[5]]
        + [jnp.zeros_like(kernel_in[0])] * 2
        + [kernel_in[4]],
        axis=1,
    )
    code = (block_index * per_device + slot_index).reshape(geometry_count, -1, NB)
    latent = []
    for geometry in range(geometry_count):
        turned = code[geometry].T
        latent.append(
            encode(
                turned % per_device,
                turned // per_device,
                counts[geometry].reshape(1, -1),
                centres,
                packed_table(table[geometry]),
                first,
                kernel_mid.T,
                kernel_out.T,
            )
        )
    latent = jnp.stack(latent)
    latent = latent.reshape(geometry_count, cells_x, cells_y, cells_z, channels)
    cos_centred, sin_centred = tables(GRID, MODES, True)
    cos_third, sin_third = tables(GRID, MODES, False)
    back_cos, back_sin = third_weights(cos_third, sin_third, GRID)
    depth_full = lax.all_to_all(latent, "gz", split_axis=4, concat_axis=3, tiled=True)
    real_part, imag_part = forward_real(
        depth_full.astype(jnp.float32), cos_third, sin_third, "gxyzc,kz->gxykc"
    )
    real_part, imag_part = (
        lax.all_to_all(real_part, "gy", split_axis=3, concat_axis=2, tiled=True),
        lax.all_to_all(imag_part, "gy", split_axis=3, concat_axis=2, tiled=True),
    )
    real_part, imag_part = forward_complex(
        real_part, imag_part, cos_centred, sin_centred, "gxykc,jy->gxjkc"
    )
    real_part, imag_part = (
        lax.all_to_all(real_part, "gx", split_axis=2, concat_axis=1, tiled=True),
        lax.all_to_all(imag_part, "gx", split_axis=2, concat_axis=1, tiled=True),
    )
    real_part, imag_part = forward_complex(
        real_part, imag_part, cos_centred, sin_centred, "gxjkc,ix->gijkc"
    )
    spec_real, spec_imag = (
        exchange(real_part, "gz", split_axis=1, concat_axis=4),
        exchange(imag_part, "gz", split_axis=1, concat_axis=4),
    )
    spec_real = spec_real.astype(jnp.bfloat16)
    spec_imag = spec_imag.astype(jnp.bfloat16)
    mixed_real = jnp.einsum(
        "gijkc,ijkco->gijko", spec_real, spectral[0], preferred_element_type=jnp.float32
    ) - jnp.einsum("gijkc,ijkco->gijko", spec_imag, spectral[1], preferred_element_type=jnp.float32)
    mixed_imag = jnp.einsum(
        "gijkc,ijkco->gijko", spec_real, spectral[1], preferred_element_type=jnp.float32
    ) + jnp.einsum("gijkc,ijkco->gijko", spec_imag, spectral[0], preferred_element_type=jnp.float32)
    first_place = (place_x + place_y + place_z) == 0
    modes = mixed_real.shape[1:4]
    order = sum(lax.broadcasted_iota(jnp.int32, modes, d) for d in range(3))
    zero_mode = ((order == 0) & first_place)[None, ..., None]
    mixed_real = jnp.where(zero_mode, 0.0, mixed_real)
    mixed_imag = jnp.where(zero_mode, 0.0, mixed_imag)
    mixed_real = mixed_real.astype(jnp.bfloat16)
    mixed_imag = mixed_imag.astype(jnp.bfloat16)
    real_part, imag_part = (
        exchange(mixed_real, "gz", split_axis=4, concat_axis=1),
        exchange(mixed_imag, "gz", split_axis=4, concat_axis=1),
    )
    real_part, imag_part = inverse_complex(
        real_part.astype(jnp.float32),
        imag_part.astype(jnp.float32),
        cos_centred,
        sin_centred,
        "gijkc,ix->gxjkc",
    )
    real_part, imag_part = (
        exchange(real_part, "gx", split_axis=1, concat_axis=2),
        exchange(imag_part, "gx", split_axis=1, concat_axis=2),
    )
    real_part, imag_part = inverse_complex(
        real_part, imag_part, cos_centred, sin_centred, "gxjkc,jy->gxykc"
    )
    real_part, imag_part = (
        exchange(real_part, "gy", split_axis=2, concat_axis=3),
        exchange(imag_part, "gy", split_axis=2, concat_axis=3),
    )
    depth_part = inverse_real(real_part, imag_part, back_cos, back_sin, "gxykc,kz->gxyzc")
    branch = exchange(depth_part, "gz", split_axis=3, concat_axis=4)
    skip = jnp.einsum("gxyzc,co->gxyzo", latent, skip_weight, preferred_element_type=jnp.float32)
    cells_total = float(GRID**3)
    variance = (
        lax.psum(jnp.sum(branch * branch, axis=(1, 2, 3)), ("gx", "gy", "gz")) / cells_total
    )
    normed = branch / jnp.sqrt(variance + NORM_FLOOR)[:, None, None, None, :]
    return jax.nn.gelu(normed + skip, approximate=True)


def solution(mesh):
    in_specs = (
        P(None, None, ("gx", "gy", "gz")),
        P(None, "gx", "gy", "gz", None),
        P(None, "gx", "gy", "gz"),
        P(),
        P(),
        P(),
        P(None, "gz", "gx", "gy", None, None),
        P(),
    )
    out_specs = P(None, "gx", "gy", "gz", None)
    return jax.shard_map(body, mesh=mesh, in_specs=in_specs, out_specs=out_specs, check_vma=False)
```

time: 1670 us -> 644 us (0.39)
  other arithmetic: 526 us -> 28.9 us
  matrix products: 405 us -> 37.8 us
  local copies, waits for them, and re-layouts: 465 us -> 110 us
  Pallas kernels: 0 us -> 286 us
  blocking collectives: 126 us -> 72.7 us
  loops' own time: 36.1 us -> 0 us
    dot_general x68 -> x20, matrix products: 390 us -> 23 us  [contract(): return jnp.einsum(pattern, operand, table, precision=HIGH)]
    pallas_call x0 -> x1, Pallas kernels: none -> 286 us  [encode(): pl.pallas_call(functools.partial(encoder_kernel, 27), grid=(nodes // widt...]
    add x17 -> x1, other arithmetic: 268 us -> 14 us  [body(): block_index * per_device + slot_index]
    reduce_sum x34 -> x2, other arithmetic: 213 us -> 3.52 us  [body(): jnp.sum(branch * branch, axis=(1, 2, 3))]
    add x18 -> x0, local copies, waits for them, and re-layouts: 165 us -> none  [the longest x16 161 us: one_slab(): found = found[0] + found[1] + found[2]]
    dot_general x16 -> x0, local copies, waits for them, and re-layouts: 110 us -> none  [kernel_mean(): jnp.dot(kernel_out.T, hidden_two, preferred_element_type=jnp.float32)]
    all_to_all x13 -> x12, local copies, waits for them, and re-layouts: 46.1 us -> 4.39 us  [exchange(): lax.all_to_all(values.astype(jnp.bfloat16), axis, split_axis=split_axis,...]
    psum x2 -> x1, blocking collectives: 79.4 us -> 38.5 us  [body(): lax.psum(jnp.sum(branch * branch, axis=(1, 2, 3)), ('gx', 'gy', 'gz'))]
  transfers between devices with their start and end apart: 18 -> 18, of which waited for: 12 -> 12; matrix products, arithmetic and copies ran while one was open for 4% -> 9% of each run, Pallas kernels for 0% -> 0%
where the time goes in v1:
time: 644 us; the launch traced here: 634 us
  Pallas kernels  286 us (44%)
  local copies, waits for them, and re-layouts  110 us (17%)
  blocking collectives  72.7 us (11%)
  starting transfers between devices  59.9 us (9%)
  matrix products  37.8 us (6%)
  waiting for transfers between devices  37.6 us (6%)
  other arithmetic  28.9 us (4%)
    pallas_call x1, Pallas kernels, encode(): pl.pallas_call(functools.partial(encoder_kernel, 27), grid=(nodes // widt...  286 us
    unnamed x43, local copies, waits for them, and re-layouts  39.1 us
    psum x1, blocking collectives, body(): lax.psum(jnp.sum(branch * branch, axis=(1, 2, 3)), ('gx', 'gy', 'gz'))  38.5 us
    all_to_all x8, starting transfers between devices, exchange(): lax.all_to_all(values.astype(jnp.bfloat16), axis, split_axis=split_axis,...  26.7 us
    all_to_all x8, waiting for transfers between devices, exchange(): lax.all_to_all(values.astype(jnp.bfloat16), axis, split_axis=split_axis,...  23 us
    dot_general x20, matrix products, contract(): return jnp.einsum(pattern, operand, table, precision=HIGH)  23 us
    convert_element_type x2, local copies, waits for them, and re-layouts, exchange(): return lax.all_to_all(values.astype(jnp.bfloat16), axis, split_axis=split...  18.7 us
    all_to_all x1, blocking collectives, body(): lax.all_to_all(latent, 'gz', split_axis=4, concat_axis=3, tiled=True)  17.9 us
  transfers between devices with their start and end apart: 18, of which 12 were waited for; matrix products, arithmetic and copies ran while one was open for 9% of the time, Pallas kernels for 0%

profile of v1, /device:TPU:0, one launch (start us, length us, event | category | flops | bytes accessed | tf_op | source)
XLA Modules:
  0.0 634.1 jit_solution(9530861041142679091)
XLA Ops:
  1.4 5.6 collective-permute-start
  7.1 14.0 %fusion.8 = s32[1,16,16,32,32]{4,3,2,1,0:T(8,128)} fusion(s32[1,16,16,32,32]{4,3,2,1,0:T(8,128)} %param.9, s32[]{:T(128)S(6)} %axis_index.38, s32[]{:T(128)S(6)} %axis_index.36, s32[]{:T(128)S(6)} %axis_index.33), kind=kLoop, calls=%fused_computation.27 | loop fusion | flops 18612224 | bytes 2097164 | tf_op jit(solution)/shard_map/add | solution.py:206
  33.3 4.6 collective-permute-start.4
  42.9 286.2 %shard_map.82 = bf16[8192,64]{1,0:T(8,128)(2,1)} custom-call(s32[32,8192]{1,0:T(8,128)} %get-tuple-element.8.slots_ref, s32[32,8192]{1,0:T(8,128)} %get-tuple-element.7.blocks_ref, s32[1,8192]{1,0:T(1,128)} %reshape_squeeze.3.counts_ref, f32[8,8192]{1,0:T(8,128)} %select_maximum_fusion.centres_ref, bf16[256,512]{1,0:T(8,128)(2,1)} %fusion.63.table_ref, ...), custom_call_target="tpu_custom_call" | custom-call | tf_op jit(solution)/shard_map/pallas_call | solution.py:138
  329.1 7.7 %copy.122 = bf16[1,16,16,32,64]{3,2,1,0,4:T(8,128)(2,1)} copy(bf16[1,16,16,32,64]{4,3,2,1,0:T(8,128)(2,1)} %bitcast.343) | data formatting | bytes 2097152 | tf_op jit(solution)/shard_map/reshape;stack | solution.py:223
  336.7 5.7 reshape.253
  342.4 17.9 %all_to_all.204 = bf16[2,2,131072]{2,1,0:T(2,128)(2,1)S(1)} all-to-all(bf16[2,2,131072]{2,1,0:T(2,128)(2,1)S(1)} %reshape.253), channel_id=1, replica_groups=mesh['gx'=4,'gy'=4,'gz'=2] {'gz'}, dimensions={0} | all-to-all | bytes 2097152 | tf_op jit(solution)/shard_map/all_to_all | solution.py:227
  363.6 8.5 %copy.229 = bf16[1,16,16,32,2,32]{3,4,5,2,1,0:T(2,128)(2,1)} copy(bf16[1,16,16,32,2,32]{3,2,1,5,4,0:T(8,128)(2,1)} %bitcast.340) | data formatting | bytes 2097152 | tf_op jit(solution)/shard_map/all_to_all | solution.py:227
  372.0 6.8 %reshape.222 = bf16[16,16,64,32]{2,3,1,0:T(8,128)(2,1)S(1)} reshape(bf16[1,16,16,2,32,32]{4,3,5,2,1,0:T(2,128)(2,1)} %bitcast.342) | data formatting | bytes 2097152 | tf_op jit(solution)/shard_map/reshape.2
  378.8 5.6 convolution_bitcast_fusion
  392.9 5.5 negate_bitcast_fusion
  401.6 4.1 all-to-all-start.2
  425.5 4.8 all-to-all-start.4
  432.2 4.0 all-to-all-done.4
  441.1 4.3 all-to-all-done.3
  491.9 4.2 all-to-all-done.10
  500.0 5.2 all-to-all-done.9
  535.0 6.8 %copy.161 = bf16[1,16,16,64,32]{4,2,1,0,3:T(8,128)(2,1)} copy(bf16[1,16,16,64,32]{3,4,2,1,0:T(8,128)(2,1)S(1)} %fusion.37) | data formatting | bytes 2097152 | tf_op jit(solution)/shard_map/convert_element_type | solution.py:159
  541.8 5.7 reshape.279
  547.4 16.3 %all_to_all.205 = bf16[2,2,131072]{2,1,0:T(2,128)(2,1)S(1)} all-to-all(bf16[2,2,131072]{2,1,0:T(2,128)(2,1)S(1)} %reshape.279), channel_id=1, replica_groups=mesh['gx'=4,'gy'=4,'gz'=2] {'gz'}, dimensions={0} | all-to-all | bytes 2097152 | tf_op jit(solution)/shard_map/all_to_all | solution.py:158
  570.6 38.5 %psum.7 = f32[1,64]{1,0:T(1,128)S(1)} all-reduce(f32[1,64]{1,0:T(1,128)S(1)} %reduce_sum.21), channel_id=1, replica_groups=mesh['gx'=4,'gy'=4,'gz'=2] {'gx','gy','gz'}, use_global_device_ids=true, to_apply=%region_2.3 | all-reduce | flops 64 | bytes 512 | tf_op jit(solution)/shard_map/psum | solution.py:292
  609.1 9.8 %copy.228 = f32[1,16,16,2,32,32]{5,3,4,2,1,0:T(2,128)} copy(bf16[1,16,16,2,32,32]{5,2,1,4,3,0:T(8,128)(2,1)} %bitcast.332) | data formatting | bytes 3145728 | tf_op jit(solution)/shard_map/convert_element_type | solution.py:160
  618.9 9.0 %reshape.236 = f32[16,16,32,64]{3,2,1,0:T(8,128)} reshape(f32[1,16,16,32,2,32]{5,4,3,2,1,0:T(2,128)} %bitcast.333) | data formatting | bytes 4194304 | tf_op jit(solution)/shard_map/convert_element_type | solution.py:160
  627.8 5.8 fusion.21
  (164 shorter events, 146.5 us)
Async XLA Ops:
  0.0 627.8 %copy-start = (bf16[64,64]{1,0:T(8,128)(2,1)S(1)}, bf16[64,64]{1,0:T(8,128)(2,1)}, u32[]{:S(2)}) copy-start(bf16[64,64]{1,0:T(8,128)(2,1)} %param.15) | copy-start | bytes 24580
  0.0 26.7 %collective-permute-start.1 = (f32[1,1,1,1,6,512]{5,0,4,3,2,1:T(1,128)}, f32[1,1,1,1,6,512]{5,0,4,3,2,1:T(1,128)S(1)}, u32[]{:S(2)}, u32[]{:S(2)}) collective-permute-start(f32[1,1,1,1,6,512]{5,0,4,3,2,1:T(1,128)} %bitcast.391), channel_id=1, source_target_pairs={{8,0},{16,8},{24,16},{9,1},{17,9},{25,17},{10,2},{18,10},{26,18},{... | collective-permute-start | bytes 36872 | tf_op jit(solution)/shard_map/ppermute | solution.py:30
  1.4 25.3 %collective-permute-start = (f32[1,1,1,1,6,512]{5,0,4,3,2,1:T(1,128)}, f32[1,1,1,1,6,512]{5,0,4,3,2,1:T(1,128)S(1)}, u32[]{:S(2)}, u32[]{:S(2)}) collective-permute-start(f32[1,1,1,1,6,512]{5,0,4,3,2,1:T(1,128)} %bitcast.392), channel_id=1, source_target_pairs={{0,8},{8,16},{16,24},{1,9},{9,17},{17,25},{2,10},{10,18},{18,26},{... | collective-permute-start | bytes 36872 | tf_op jit(solution)/shard_map/ppermute | solution.py:28
  21.1 5.7 copy-start.4
  21.1 16.8 %copy-start.6 = (bf16[6,80]{1,0:T(8,128)(2,1)S(1)}, bf16[6,80]{1,0:T(8,128)(2,1)}, u32[]{:S(2)}) copy-start(bf16[6,80]{1,0:T(8,128)(2,1)} %param.11) | copy-start | bytes 2884
  21.1 17.6 %copy-start.5 = (bf16[80,80]{1,0:T(8,128)(2,1)S(1)}, bf16[80,80]{1,0:T(8,128)(2,1)}, u32[]{:S(2)}) copy-start(bf16[80,80]{1,0:T(8,128)(2,1)} %param.12) | copy-start | bytes 38404
  21.1 18.3 %copy-start.3 = (s32[1,16,16,32]{3,2,1,0:T(8,128)S(1)}, s32[1,16,16,32]{3,2,1,0:T(8,128)}, u32[]{:S(2)}) copy-start(s32[1,16,16,32]{3,2,1,0:T(8,128)} %param.10) | copy-start | bytes 98308
  26.8 5.2 collective-permute-start.3
  28.1 3.9 collective-permute-start.2
  32.0 8.1 %collective-permute-start.5 = (f32[3,3,1,1,6,512]{5,0,4,3,2,1:T(4,128)S(1)}, f32[3,3,1,1,6,512]{5,0,4,3,2,1:T(4,128)S(1)}, u32[]{:S(2)}, u32[]{:S(2)}) collective-permute-start(f32[3,3,1,1,6,512]{5,0,4,3,2,1:T(4,128)S(1)} %pad_maximum_fusion), channel_id=1, source_target_pairs={{1,0},{3,2},{5,4},{7,6},{9,8},{11,10},{13,12},{15,14},{17,16},{19,... | collective-permute-start | bytes 331784 | tf_op jit(solution)/shard_map/ppermute | solution.py:30
  33.3 8.2 %collective-permute-start.4 = (f32[3,3,1,1,6,512]{5,0,4,3,2,1:T(4,128)S(1)}, f32[3,3,1,1,6,512]{5,0,4,3,2,1:T(4,128)S(1)}, u32[]{:S(2)}, u32[]{:S(2)}) collective-permute-start(f32[3,3,1,1,6,512]{5,0,4,3,2,1:T(4,128)S(1)} %pad_maximum_fusion), channel_id=1, source_target_pairs={{0,1},{2,3},{4,5},{6,7},{8,9},{10,11},{12,13},{14,15},{16,17},{18,... | collective-permute-start | bytes 331784 | tf_op jit(solution)/shard_map/ppermute | solution.py:28
  389.2 12.5 %all-to-all-start.1 = ((f32[4,1,32768]{2,1,0:T(1,128)}), f32[4,1,32768]{2,1,0:T(1,128)S(1)}, u32[]{:S(2)}, u32[]{:S(2)}) async-start(f32[4,1,32768]{2,1,0:T(1,128)} %reshape.257), calls=%async_computation.1 | async-start | bytes 1048576 | tf_op jit(solution)/shard_map/all_to_all | solution.py:232
  401.6 13.0 %all-to-all-start.2 = ((f32[4,1,32768]{2,1,0:T(1,128)}), f32[4,1,32768]{2,1,0:T(1,128)}, u32[]{:S(2)}, u32[]{:S(2)}) async-start(f32[4,1,32768]{2,1,0:T(1,128)} %reshape.255), calls=%async_computation.2 | async-start | bytes 1048576 | tf_op jit(solution)/shard_map/all_to_all | solution.py:233
  425.5 10.8 %all-to-all-start.4 = ((f32[4,1,8192]{2,1,0:T(1,128)}), f32[4,1,8192]{2,1,0:T(1,128)S(1)}, u32[]{:S(2)}, u32[]{:S(2)}) async-start(f32[4,1,8192]{2,1,0:T(1,128)} %reshape.259), calls=%async_computation.4 | async-start | bytes 262144 | tf_op jit(solution)/shard_map/all_to_all | solution.py:240
  436.2 9.2 %all-to-all-start.3 = ((f32[4,1,8192]{2,1,0:T(1,128)}), f32[4,1,8192]{2,1,0:T(1,128)S(1)}, u32[]{:S(2)}, u32[]{:S(2)}) async-start(f32[4,1,8192]{2,1,0:T(1,128)} %reshape.261), calls=%async_computation.3 | async-start | bytes 262144 | tf_op jit(solution)/shard_map/all_to_all | solution.py:239
  448.2 7.1 %all-to-all-start.6 = ((bf16[2,2,2048]{2,1,0:T(2,128)(2,1)}), bf16[2,2,2048]{2,1,0:T(2,128)(2,1)S(1)}, u32[]{:S(2)}, u32[]{:S(2)}) async-start(bf16[2,2,2048]{2,1,0:T(2,128)(2,1)} %reshape.263), calls=%async_computation.6 | async-start | bytes 32768 | tf_op jit(solution)/shard_map/all_to_all | solution.py:158
  455.2 8.0 %all-to-all-start.5 = ((bf16[2,2,2048]{2,1,0:T(2,128)(2,1)}), bf16[2,2,2048]{2,1,0:T(2,128)(2,1)S(1)}, u32[]{:S(2)}, u32[]{:S(2)}) async-start(bf16[2,2,2048]{2,1,0:T(2,128)(2,1)} %reshape.265), calls=%async_computation.5 | async-start | bytes 32768 | tf_op jit(solution)/shard_map/all_to_all | solution.py:158
  470.7 7.1 %all-to-all-start.7 = ((bf16[2,2,2048]{2,1,0:T(2,128)(2,1)}), bf16[2,2,2048]{2,1,0:T(2,128)(2,1)S(1)}, u32[]{:S(2)}, u32[]{:S(2)}) async-start(bf16[2,2,2048]{2,1,0:T(2,128)(2,1)} %reshape.267), calls=%async_computation.7 | async-start | bytes 32768 | tf_op jit(solution)/shard_map/all_to_all | solution.py:158
  477.8 7.1 %all-to-all-start.8 = ((bf16[2,2,2048]{2,1,0:T(2,128)(2,1)}), bf16[2,2,2048]{2,1,0:T(2,128)(2,1)S(1)}, u32[]{:S(2)}, u32[]{:S(2)}) async-start(bf16[2,2,2048]{2,1,0:T(2,128)(2,1)} %reshape.269), calls=%async_computation.8 | async-start | bytes 32768 | tf_op jit(solution)/shard_map/all_to_all | solution.py:158
  487.1 9.0 %all-to-all-start.10 = ((bf16[4,2,4096]{2,1,0:T(2,128)(2,1)}), bf16[4,2,4096]{2,1,0:T(2,128)(2,1)S(1)}, u32[]{:S(2)}, u32[]{:S(2)}) async-start(bf16[4,2,4096]{2,1,0:T(2,128)(2,1)} %reshape.273), calls=%async_computation.10 | async-start | bytes 131072 | tf_op jit(solution)/shard_map/all_to_all | solution.py:158
  496.1 9.2 %all-to-all-start.9 = ((bf16[4,2,4096]{2,1,0:T(2,128)(2,1)}), bf16[4,2,4096]{2,1,0:T(2,128)(2,1)S(1)}, u32[]{:S(2)}, u32[]{:S(2)}) async-start(bf16[4,2,4096]{2,1,0:T(2,128)(2,1)} %reshape.271), calls=%async_computation.9 | async-start | bytes 131072 | tf_op jit(solution)/shard_map/all_to_all | solution.py:158
  510.2 9.4 %all-to-all-start.12 = ((bf16[4,2,16384]{2,1,0:T(2,128)(2,1)}), bf16[4,2,16384]{2,1,0:T(2,128)(2,1)S(1)}, u32[]{:S(2)}, u32[]{:S(2)}) async-start(bf16[4,2,16384]{2,1,0:T(2,128)(2,1)} %reshape.277), calls=%async_computation.12 | async-start | bytes 524288 | tf_op jit(solution)/shard_map/all_to_all | solution.py:158
  519.6 9.6 %all-to-all-start.11 = ((bf16[4,2,16384]{2,1,0:T(2,128)(2,1)}), bf16[4,2,16384]{2,1,0:T(2,128)(2,1)S(1)}, u32[]{:S(2)}, u32[]{:S(2)}) async-start(bf16[4,2,16384]{2,1,0:T(2,128)(2,1)} %reshape.275), calls=%async_computation.11 | async-start | bytes 524288 | tf_op jit(solution)/shard_map/all_to_all | solution.py:158
  618.9 9.0 %copy-start.2 = (bf16[8192,64]{1,0:T(8,128)(2,1)S(1)}, bf16[8192,64]{1,0:T(8,128)(2,1)}, u32[]{:S(2)}) copy-start(bf16[8192,64]{1,0:T(8,128)(2,1)} %shard_map.82) | copy-start | bytes 3145732
  (1 other events, 2.2 us)
